TPU v7x, 256 devices: a whole 4x4x8 slice. The times are simulated.
256 devices in a mesh: trial: 4 (over z_lo), ep: 4 (over y), fsdp: 16 (over z_hi, x, core).
Axes of the slice: x: 4, y: 4, z: 8 (z_hi: 2, z_lo: 4; z = z_hi * 4 + z_lo), core: 2. Of those that a mesh axis runs over, the one named last changes fastest.
Arguments:
- master_down: float32 [256, 1024, 2048], P(('trial', 'ep'), None, 'fsdp'), parts along dimension 0, may hold values from -0.25 to 0.25
- router_weight: float32 [8192, 64], P(('trial', 'fsdp'), 'ep'), parts along dimension 0, may hold values from -0.125 to 0.125
- router_gain: float32 [8192], P(('trial', 'fsdp')), parts along dimension 0, may hold values from 0.25 to 1.75
Outputs:
- final_down: bfloat16 [256, 1024, 2048], P(('trial', 'ep'), 'fsdp'), parts along dimension 0
- scale_down: float32 [256, 1024], P(('trial', 'ep'), 'fsdp'), parts along dimension 0
- serve_router: bfloat16 [8192, 64], P('trial'), parts along dimension 0
There are 4 independent parts, one for each index of `trial`. A program takes and returns all parts, laid end to end along the dimension named above; each array names one. Nothing has to cross between parts.
All inputs are finite; a program needn't handle non-finite values. Where the computation divides by a largest or mean magnitude, that divisor is 1e-20 or more.
Results may differ from a plain program's by a relative error of at most 0.001.
Values may be sent and summed in bfloat16 or wider, within the bound.
A program may use at most 64 MiB of HBM per device.

v0:
```python
import jax
import jax.numpy as jnp
from jax import lax
from jax.sharding import PartitionSpec as P


def copy_for_each(shard, axis):
    copies = jnp.broadcast_to(shard, (lax.axis_size(axis), *shard.shape))
    return lax.all_to_all(copies, axis, split_axis=0, concat_axis=0, tiled=True)


def taken_together(shard, axis):
    return copy_for_each(shard, axis).max(axis=0)


def laid_out(blocks, dim):
    lengths = list(blocks.shape[1:])
    lengths[dim] *= blocks.shape[0]
    return jnp.moveaxis(blocks, 0, dim).reshape(lengths)


def gathered_copies(shard, axis, dim):
    blocks = copy_for_each(shard, axis)
    return laid_out(blocks, dim)


def shards(master_down, router_weight, router_gain):
    scale_down = taken_together(jnp.max(jnp.abs(master_down), axis=2), "fsdp")
    narrow_down = (master_down / jnp.expand_dims(scale_down, 2)).astype(jnp.bfloat16)
    final_down = lax.all_to_all(narrow_down, "fsdp", split_axis=1, concat_axis=2, tiled=True)
    scale_down = lax.dynamic_slice_in_dim(
        scale_down, lax.axis_index("fsdp") * final_down.shape[1], final_down.shape[1], axis=1
    )
    part_router = (router_weight * router_gain[:, None]).astype(jnp.bfloat16)
    row_router = gathered_copies(part_router, "fsdp", 0)
    serve_router = lax.all_gather(row_router, "ep", axis=1, tiled=True)
    return (final_down, scale_down, serve_router)


def solution(mesh):
    return jax.shard_map(
        shards,
        mesh=mesh,
        in_specs=(
            P(("trial", "ep"), None, "fsdp"),
            P(("trial", "fsdp"), "ep"),
            P(("trial", "fsdp")),
        ),
        out_specs=(P(("trial", "ep"), "fsdp", None), P(("trial", "ep"), "fsdp"), P("trial", None)),
        check_vma=False,
    )
```

profile of v0, /device:TPU:55, one launch (start us, length us, event | category | flops | bytes accessed | tf_op | source)
XLA Modules:
  0.0 194.5 jit_solution(12414777083532193542)
XLA Ops:
  0.6 0.0 copy-start
  0.6 0.0 copy-start.1
  0.7 5.6 %abs_reduce_fusion = f32[16,1024]{1,0:T(8,128)S(1)} fusion(f32[16,1024,128]{2,1,0:T(8,128)} %param.3), kind=kLoop, calls=%fused_computation.2 | loop fusion | flops 4177920 | bytes 8454144 | tf_op jit(solution)/shard_map/reduce_max | solution.py:28
  6.3 1.1 broadcast_in_dim.8
  7.4 10.8 %all-to-all-start = ((f32[16,16,1024]{2,1,0:T(8,128)}), f32[16,16,1024]{2,1,0:T(8,128)S(1)}, u32[]{:S(2)}, u32[]{:S(2)}) async-start(f32[16,16,1024]{2,1,0:T(8,128)} %broadcast_in_dim.8), calls=%async_computation | async-start | bytes 2097152 | tf_op jit(solution)/shard_map/all_to_all | solution.py:9
  18.2 0.0 copy-done
  18.2 0.0 copy-done.1
  18.2 30.0 %all-to-all-done = f32[16,16,1024]{2,1,0:T(8,128)S(1)} async-done(((f32[16,16,1024]{2,1,0:T(8,128)}), f32[16,16,1024]{2,1,0:T(8,128)S(1)}, u32[]{:S(2)}, u32[]{:S(2)}) %all-to-all-start) | async-done | bytes 1048608 | tf_op jit(solution)/shard_map/all_to_all | solution.py:9
  48.2 0.6 broadcast_in_dim.9
  48.8 5.0 %all-to-all-start.2 = ((bf16[16,128,16]{1,2,0:T(8,128)(2,1)}), bf16[16,128,16]{1,2,0:T(8,128)(2,1)S(1)}, u32[]{:S(2)}, u32[]{:S(2)}) async-start(bf16[16,128,16]{1,2,0:T(8,128)(2,1)} %broadcast_in_dim.9), calls=%async_computation.2 | async-start | bytes 131072 | tf_op jit(solution)/shard_map/all_to_all | solution.py:9
  53.8 0.1 reduce_max.19
  53.9 0.2 copy.14
  54.1 9.6 %fusion = bf16[16,1024,128]{2,0,1:T(8,128)(2,1)} fusion(f32[16,1024,128]{2,1,0:T(8,128)} %param.3, f32[16,1024]{0,1:T(8,128)S(1)} %copy.14), kind=kLoop, calls=%fused_computation.1 | loop fusion | flops 4194304 | bytes 12648448 | tf_op jit(solution)/shard_map/convert_element_type | solution.py:29
  63.7 0.0 all-to-all-done.2
  63.7 9.7 %all-to-all-start.1 = ((bf16[16,1024,128]{2,0,1:T(8,128)(2,1)}), bf16[16,1024,128]{2,0,1:T(8,128)(2,1)}, u32[]{:S(2)}, u32[]{:S(2)}) async-start(bf16[16,1024,128]{2,0,1:T(8,128)(2,1)} %fusion), calls=%async_computation.1 | async-start | bytes 8388608 | tf_op jit(solution)/shard_map/all_to_all | solution.py:30
  73.4 9.4 %all_gather.3 = bf16[2048,64]{0,1:T(8,128)(2,1)S(1)} all-gather(bf16[2048,16]{0,1:T(8,128)(2,1)S(1)} %copy_bitcast_fusion), channel_id=1, replica_groups=mesh['trial'=4,'ep'=4,'fsdp'=16] {'ep'}, dimensions={1}, use_global_device_ids=true | all-gather | bytes 327680 | tf_op jit(solution)/shard_map/all_gather | solution.py:36
  82.7 0.7 constant_dynamic-slice_fusion
  83.4 96.2 %all-to-all-done.1 = bf16[16,1024,128]{2,0,1:T(8,128)(2,1)} async-done(((bf16[16,1024,128]{2,0,1:T(8,128)(2,1)}), bf16[16,1024,128]{2,0,1:T(8,128)(2,1)}, u32[]{:S(2)}, u32[]{:S(2)}) %all-to-all-start.1) | async-done | bytes 4194336 | tf_op jit(solution)/shard_map/all_to_all | solution.py:30
  179.7 6.9 %copy.16 = bf16[16,64,16,128]{3,2,1,0:T(8,128)(2,1)} copy(bf16[16,64,16,128]{3,0,1,2:T(8,128)(2,1)} %bitcast.1) | data formatting | bytes 8388608 | tf_op jit(solution)/shard_map/all_to_all | solution.py:30
  186.5 7.3 %all_to_all.23 = bf16[16,64,2048]{2,1,0:T(8,128)(2,1)} reshape(bf16[16,64,16,128]{3,2,1,0:T(8,128)(2,1)} %copy.16) | data formatting | bytes 8388608 | tf_op jit(solution)/shard_map/all_to_all | solution.py:30
  193.8 0.7 copy.24
  (2 shorter events, 0.0 us)
Async XLA Ops:
  0.6 17.5 %copy-start = (f32[128,16]{0,1:T(8,128)S(1)}, f32[128,16]{0,1:T(8,128)}, u32[]{:S(2)}) copy-start(f32[128,16]{0,1:T(8,128)} %param.4) | copy-start | bytes 24580
  0.6 17.5 %copy-start.1 = (f32[128]{0:T(128)S(1)}, f32[128]{0:T(128)}, u32[]{:S(2)}) copy-start(f32[128]{0:T(128)} %param.5) | copy-start | bytes 1540
  7.4 40.8 %all-to-all-start = ((f32[16,16,1024]{2,1,0:T(8,128)}), f32[16,16,1024]{2,1,0:T(8,128)S(1)}, u32[]{:S(2)}, u32[]{:S(2)}) async-start(f32[16,16,1024]{2,1,0:T(8,128)} %broadcast_in_dim.8), calls=%async_computation | async-start | bytes 2097152 | tf_op jit(solution)/shard_map/all_to_all | solution.py:9
  48.8 14.9 %all-to-all-start.2 = ((bf16[16,128,16]{1,2,0:T(8,128)(2,1)}), bf16[16,128,16]{1,2,0:T(8,128)(2,1)S(1)}, u32[]{:S(2)}, u32[]{:S(2)}) async-start(bf16[16,128,16]{1,2,0:T(8,128)(2,1)} %broadcast_in_dim.9), calls=%async_computation.2 | async-start | bytes 131072 | tf_op jit(solution)/shard_map/all_to_all | solution.py:9
  63.7 115.9 %all-to-all-start.1 = ((bf16[16,1024,128]{2,0,1:T(8,128)(2,1)}), bf16[16,1024,128]{2,0,1:T(8,128)(2,1)}, u32[]{:S(2)}, u32[]{:S(2)}) async-start(bf16[16,1024,128]{2,0,1:T(8,128)(2,1)} %fusion), calls=%async_computation.1 | async-start | bytes 8388608 | tf_op jit(solution)/shard_map/all_to_all | solution.py:30
where the time goes:
time: 195 us; the launch traced here: 194 us
  waiting for transfers between devices  126 us (65%)
  starting transfers between devices  25.5 us (13%)
  local copies, waits for them, and re-layouts  17.4 us (9%)
  other arithmetic  15.3 us (8%)
  blocking collectives  9.36 us (5%)
    all_to_all x1, waiting for transfers between devices, shards(): lax.all_to_all(narrow_down, 'fsdp', split_axis=1, concat_axis=2, tiled=True)  96.2 us
    all_to_all x2, waiting for transfers between devices, copy_for_each(): return lax.all_to_all(copies, axis, split_axis=0, concat_axis=0, tiled=True)  30 us
    all_to_all x2, starting transfers between devices, copy_for_each(): return lax.all_to_all(copies, axis, split_axis=0, concat_axis=0, tiled=True)  15.8 us
    all_to_all x2, local copies, waits for them, and re-layouts, shards(): lax.all_to_all(narrow_down, 'fsdp', split_axis=1, concat_axis=2, tiled=True)  14.1 us
    all_to_all x1, starting transfers between devices, shards(): lax.all_to_all(narrow_down, 'fsdp', split_axis=1, concat_axis=2, tiled=True)  9.66 us
    convert_element_type x1, other arithmetic, shards(): (master_down / jnp.expand_dims(scale_down, 2)).astype(jnp.bfloat16)  9.63 us
    all_gather x1, blocking collectives, shards(): serve_router = lax.all_gather(row_router, 'ep', axis=1, tiled=True)  9.36 us
    reduce_max x1, other arithmetic, shards(): scale_down = taken_together(jnp.max(jnp.abs(master_down), axis=2), 'fsdp')  5.62 us
  transfers between devices with their start and end apart: 3, of which 2 were waited for; matrix products, arithmetic and copies ran while one was open for 5% of the time, Pallas kernels for 0%

commit v1 on v0

--- a/solution.py
+++ b/solution.py
@@ -33,7 +33,10 @@
     )
     part_router = (router_weight * router_gain[:, None]).astype(jnp.bfloat16)
     row_router = gathered_copies(part_router, "fsdp", 0)
-    serve_router = lax.all_gather(row_router, "ep", axis=1, tiled=True)
+    size = lax.axis_size("ep")
+    pieces = jnp.stack([row_router for _ in range(size)])
+    pieces = lax.all_to_all(pieces, "ep", split_axis=0, concat_axis=0)
+    serve_router = jnp.concatenate(pieces, axis=1)
     return (final_down, scale_down, serve_router)
 
 

time: 195 us -> 201 us (1.031)
  waiting for transfers between devices: 126 us -> 137 us
  blocking collectives: 9.36 us -> 0 us
  starting transfers between devices: 25.5 us -> 28.7 us
    all_gather x1 -> x0, blocking collectives: 9.36 us -> none  [shards(): serve_router = lax.all_gather(row_router, 'ep', axis=1, tiled=True)]
    all_to_all x1, waiting for transfers between devices: 96.2 us -> 104 us  [shards(): lax.all_to_all(narrow_down, 'fsdp', split_axis=1, concat_axis=2, tiled=True)]
    all_to_all x0 -> x1, starting transfers between devices: none -> 4.24 us  [shards(): pieces = lax.all_to_all(pieces, 'ep', split_axis=0, concat_axis=0)]
    all_to_all x1, starting transfers between devices: 9.66 us -> 6.55 us  [shards(): lax.all_to_all(narrow_down, 'fsdp', split_axis=1, concat_axis=2, tiled=True)]
    all_to_all x2, waiting for transfers between devices: 30 us -> 32.6 us  [copy_for_each(): return lax.all_to_all(copies, axis, split_axis=0, concat_axis=0, tiled=True)]
    all_to_all x2, starting transfers between devices: 15.8 us -> 17.9 us  [copy_for_each(): return lax.all_to_all(copies, axis, split_axis=0, concat_axis=0, tiled=True)]
  transfers between devices with their start and end apart: 3 -> 4, of which waited for: 2 -> 3; matrix products, arithmetic and copies ran while one was open for 5% -> 8% of each run, Pallas kernels for 0% -> 0%
where the time goes in v1:
time: 201 us; the launch traced here: 200 us
  waiting for transfers between devices  137 us (68%)
  starting transfers between devices  28.7 us (14%)
  local copies, waits for them, and re-layouts  18.2 us (9%)
  other arithmetic  16 us (8%)
    all_to_all x1, waiting for transfers between devices, shards(): lax.all_to_all(narrow_down, 'fsdp', split_axis=1, concat_axis=2, tiled=True)  104 us
    all_to_all x2, waiting for transfers between devices, copy_for_each(): return lax.all_to_all(copies, axis, split_axis=0, concat_axis=0, tiled=True)  32.6 us
    all_to_all x2, starting transfers between devices, copy_for_each(): return lax.all_to_all(copies, axis, split_axis=0, concat_axis=0, tiled=True)  17.9 us
    all_to_all x2, local copies, waits for them, and re-layouts, shards(): lax.all_to_all(narrow_down, 'fsdp', split_axis=1, concat_axis=2, tiled=True)  14.1 us
    convert_element_type x1, other arithmetic, shards(): (master_down / jnp.expand_dims(scale_down, 2)).astype(jnp.bfloat16)  9.63 us
    all_to_all x1, starting transfers between devices, shards(): lax.all_to_all(narrow_down, 'fsdp', split_axis=1, concat_axis=2, tiled=True)  6.55 us
    reduce_max x1, other arithmetic, shards(): scale_down = taken_together(jnp.max(jnp.abs(master_down), axis=2), 'fsdp')  5.61 us
    all_to_all x1, starting transfers between devices, shards(): pieces = lax.all_to_all(pieces, 'ep', split_axis=0, concat_axis=0)  4.24 us
  transfers between devices with their start and end apart: 4, of which 3 were waited for; matrix products, arithmetic and copies ran while one was open for 8% of the time, Pallas kernels for 0%

profile of v1, /device:TPU:55, one launch (start us, length us, event | category | flops | bytes accessed | tf_op | source)
XLA Modules:
  0.0 200.3 jit_solution(6867620111525462243)
XLA Ops:
  0.6 0.7 multiply_convert_fusion
  1.3 0.6 broadcast_in_dim.9
  2.0 10.8 %all-to-all-start.2 = ((bf16[16,128,16]{1,2,0:T(8,128)(2,1)}), bf16[16,128,16]{1,2,0:T(8,128)(2,1)S(1)}, u32[]{:S(2)}, u32[]{:S(2)}) async-start(bf16[16,128,16]{1,2,0:T(8,128)(2,1)} %broadcast_in_dim.9), calls=%async_computation.2 | async-start | bytes 131072 | tf_op jit(solution)/shard_map/all_to_all | solution.py:9
  12.8 5.6 %abs_reduce_fusion = f32[16,1024]{1,0:T(8,128)S(1)} fusion(f32[16,1024,128]{2,1,0:T(8,128)} %param.3), kind=kLoop, calls=%fused_computation.2 | loop fusion | flops 4177920 | bytes 8454144 | tf_op jit(solution)/shard_map/reduce_max | solution.py:28
  18.4 2.6 %all-to-all-done.2 = bf16[16,128,16]{1,2,0:T(8,128)(2,1)S(1)} async-done(((bf16[16,128,16]{1,2,0:T(8,128)(2,1)}), bf16[16,128,16]{1,2,0:T(8,128)(2,1)S(1)}, u32[]{:S(2)}, u32[]{:S(2)}) %all-to-all-start.2) | async-done | bytes 65568 | tf_op jit(solution)/shard_map/all_to_all | solution.py:9
  21.0 1.1 broadcast_in_dim.8
  22.1 7.1 %all-to-all-start = ((f32[16,16,1024]{2,1,0:T(8,128)}), f32[16,16,1024]{2,1,0:T(8,128)S(1)}, u32[]{:S(2)}, u32[]{:S(2)}) async-start(f32[16,16,1024]{2,1,0:T(8,128)} %broadcast_in_dim.8), calls=%async_computation | async-start | bytes 2097152 | tf_op jit(solution)/shard_map/all_to_all | solution.py:9
  29.1 30.0 %all-to-all-done = f32[16,16,1024]{2,1,0:T(8,128)S(1)} async-done(((f32[16,16,1024]{2,1,0:T(8,128)}), f32[16,16,1024]{2,1,0:T(8,128)S(1)}, u32[]{:S(2)}, u32[]{:S(2)}) %all-to-all-start) | async-done | bytes 1048608 | tf_op jit(solution)/shard_map/all_to_all | solution.py:9
  59.1 0.7 stack.3
  59.8 4.2 %all-to-all-start.3 = ((bf16[4,2048,16]{1,2,0:T(8,128)(2,1)}), bf16[4,2048,16]{1,2,0:T(8,128)(2,1)S(1)}, u32[]{:S(2)}, u32[]{:S(2)}) async-start(bf16[4,2048,16]{1,2,0:T(8,128)(2,1)} %stack.3), calls=%async_computation.3 | async-start | bytes 524288 | tf_op jit(solution)/shard_map/all_to_all | solution.py:38
  64.1 0.1 reduce_max.19
  64.1 0.2 copy.14
  64.3 9.6 %fusion = bf16[16,1024,128]{2,0,1:T(8,128)(2,1)} fusion(f32[16,1024,128]{2,1,0:T(8,128)} %param.3, f32[16,1024]{0,1:T(8,128)S(1)} %copy.14), kind=kLoop, calls=%fused_computation.1 | loop fusion | flops 4194304 | bytes 12648448 | tf_op jit(solution)/shard_map/convert_element_type | solution.py:29
  74.0 0.0 all-to-all-done.3
  74.0 6.5 %all-to-all-start.1 = ((bf16[16,1024,128]{2,0,1:T(8,128)(2,1)}), bf16[16,1024,128]{2,0,1:T(8,128)(2,1)}, u32[]{:S(2)}, u32[]{:S(2)}) async-start(bf16[16,1024,128]{2,0,1:T(8,128)(2,1)} %fusion), calls=%async_computation.1 | async-start | bytes 8388608 | tf_op jit(solution)/shard_map/all_to_all | solution.py:30
  80.5 0.7 constant_dynamic-slice_fusion
  81.2 104.3 %all-to-all-done.1 = bf16[16,1024,128]{2,0,1:T(8,128)(2,1)} async-done(((bf16[16,1024,128]{2,0,1:T(8,128)(2,1)}), bf16[16,1024,128]{2,0,1:T(8,128)(2,1)}, u32[]{:S(2)}, u32[]{:S(2)}) %all-to-all-start.1) | async-done | bytes 4194336 | tf_op jit(solution)/shard_map/all_to_all | solution.py:30
  185.5 6.9 %copy.16 = bf16[16,64,16,128]{3,2,1,0:T(8,128)(2,1)} copy(bf16[16,64,16,128]{3,0,1,2:T(8,128)(2,1)} %bitcast.1) | data formatting | bytes 8388608 | tf_op jit(solution)/shard_map/all_to_all | solution.py:30
  192.4 7.3 %all_to_all.26 = bf16[16,64,2048]{2,1,0:T(8,128)(2,1)} reshape(bf16[16,64,16,128]{3,2,1,0:T(8,128)(2,1)} %copy.16) | data formatting | bytes 8388608 | tf_op jit(solution)/shard_map/all_to_all | solution.py:30
  199.6 0.7 copy.24
  (1 shorter events, 0.0 us)
Async XLA Ops:
  2.0 19.0 %all-to-all-start.2 = ((bf16[16,128,16]{1,2,0:T(8,128)(2,1)}), bf16[16,128,16]{1,2,0:T(8,128)(2,1)S(1)}, u32[]{:S(2)}, u32[]{:S(2)}) async-start(bf16[16,128,16]{1,2,0:T(8,128)(2,1)} %broadcast_in_dim.9), calls=%async_computation.2 | async-start | bytes 131072 | tf_op jit(solution)/shard_map/all_to_all | solution.py:9
  22.1 37.1 %all-to-all-start = ((f32[16,16,1024]{2,1,0:T(8,128)}), f32[16,16,1024]{2,1,0:T(8,128)S(1)}, u32[]{:S(2)}, u32[]{:S(2)}) async-start(f32[16,16,1024]{2,1,0:T(8,128)} %broadcast_in_dim.8), calls=%async_computation | async-start | bytes 2097152 | tf_op jit(solution)/shard_map/all_to_all | solution.py:9
  59.8 14.1 %all-to-all-start.3 = ((bf16[4,2048,16]{1,2,0:T(8,128)(2,1)}), bf16[4,2048,16]{1,2,0:T(8,128)(2,1)S(1)}, u32[]{:S(2)}, u32[]{:S(2)}) async-start(bf16[4,2048,16]{1,2,0:T(8,128)(2,1)} %stack.3), calls=%async_computation.3 | async-start | bytes 524288 | tf_op jit(solution)/shard_map/all_to_all | solution.py:38
  74.0 111.5 %all-to-all-start.1 = ((bf16[16,1024,128]{2,0,1:T(8,128)(2,1)}), bf16[16,1024,128]{2,0,1:T(8,128)(2,1)}, u32[]{:S(2)}, u32[]{:S(2)}) async-start(bf16[16,1024,128]{2,0,1:T(8,128)(2,1)} %fusion), calls=%async_computation.1 | async-start | bytes 8388608 | tf_op jit(solution)/shard_map/all_to_all | solution.py:30
